TPU v7x, 32 devices: a whole 2x2x4 slice. The times are simulated.
32 devices in a mesh: head: 4 (over y, core), seq: 8 (over z, x).
Axes of the slice: x: 2, y: 2, z: 4, core: 2. Of those that a mesh axis runs over, the one named last changes fastest.
Arguments:
- cached_keys: bfloat16 [8, 32768, 8, 128], P(None, 'seq', 'head'), may hold values from -6 to 6
- queries: bfloat16 [8, 64, 128], P('seq', 'head'), may hold values from -6 to 6
- seq_lengths: int32 [8], replicated, may hold values from 1 to 32768
Outputs:
- page_min: bfloat16 [8, 2048, 8, 128], P('seq', 'head')
- page_max: bfloat16 [8, 2048, 8, 128], P('seq', 'head')
- page_mean: float32 [8, 2048, 8, 128], P('seq', 'head')
- page_score: float32 [8, 64, 2048], P('seq', None, 'head')
All inputs are finite; a program needn't handle non-finite values.
Results may differ from a plain program's by a relative error of at most 0.001.
Values may be sent and summed in bfloat16 or wider, within the bound.
A program may use at most 192 MiB of HBM per device.

v0:
```python
import functools

import jax
import jax.numpy as jnp
from jax import lax
from jax.experimental import pallas as pl
from jax.experimental.pallas import tpu as pltpu
from jax.sharding import PartitionSpec as P

PAGE = 16
SLOTS = 3
MESH = pl.DeviceIdType.MESH
SPAN = 28.0
TOP = 32767.0


def page_kernel(
    seqs, heads, lengths, keys, query, low_out, high_out, sum_out, query_out,
    buf, low, high, code, key_sem, send_sem, recv_sem, own_sem, query_send, query_recv, query_own,
):
    head = lax.axis_index("head")
    seq = lax.axis_index("seq")
    ratio = seqs // heads
    pages = keys.shape[1]
    width = keys.shape[3]
    lanes = keys.shape[4]
    rows = pages * width
    chunk = min(64, rows)
    owner = seq // ratio
    part = lax.rem(seq, ratio)
    mine = owner == head

    def dest_of(step):
        return lax.rem(seq + lax.rem(step + seqs // 2, seqs), seqs)

    def fetch(step):
        slot = lax.rem(step, SLOTS)
        dest = dest_of(step)
        for t in range(PAGE):
            pltpu.make_async_copy(keys.at[dest, :, t], buf.at[slot, t], key_sem.at[slot, t]).start()

    for step in range(min(SLOTS - 1, seqs)):
        fetch(jnp.int32(step))

    barrier = pltpu.get_barrier_semaphore()

    def greet(i, carry):
        source_head = i // ratio
        source_seq = head * ratio + lax.rem(i, ratio)

        @pl.when(jnp.logical_or(source_head != head, source_seq != seq))
        def _():
            pl.semaphore_signal(barrier, inc=1, device_id=(source_head, source_seq), device_id_type=MESH)

        return carry

    lax.fori_loop(0, seqs, greet, 0)
    for i in range(1, heads):
        pl.semaphore_signal(barrier, inc=1, device_id=(lax.rem(head + i, heads), seq), device_id_type=MESH)
    expected = seqs - jnp.where(mine, 1, 0) + heads - 1
    pl.semaphore_wait(barrier, expected)

    def query_copy(i, target):
        return pltpu.make_async_remote_copy(
            src_ref=query, dst_ref=query_out.at[head], send_sem=query_send.at[i], recv_sem=query_recv.at[i],
            device_id=(target, seq), device_id_type=MESH,
        )

    for i in range(heads - 1):
        query_copy(i, lax.rem(head + i + 1, heads)).start()
    own_query = pltpu.make_async_copy(query, query_out.at[head], query_own)
    own_query.start()

    trio = ((low, low_out), (high, high_out), (code, sum_out))
    index = head * ratio + part

    def remote(step, k):
        source, target = trio[k]
        return pltpu.make_async_remote_copy(
            src_ref=source.at[step],
            dst_ref=target.at[pl.ds(part * pages, pages), head],
            send_sem=send_sem.at[step, k],
            recv_sem=recv_sem.at[index, k],
            device_id=(owner, dest_of(step)),
            device_id_type=MESH,
        )

    def local(step, k):
        source, target = trio[k]
        return pltpu.make_async_copy(source.at[step], target.at[pl.ds(part * pages, pages), head], own_sem.at[k])

    def work(step, carry):
        @pl.when(step + SLOTS - 1 < seqs)
        def _():
            fetch(step + SLOTS - 1)

        slot = lax.rem(step, SLOTS)
        dest = dest_of(step)
        for t in range(PAGE):
            pltpu.make_async_copy(keys.at[dest, :, t], buf.at[slot, t], key_sem.at[slot, t]).wait()
        block = buf.at[slot]
        flat = block.reshape(PAGE, rows, lanes)
        limit = lengths[dest] - seq * (pages * PAGE)
        row = lax.broadcasted_iota(jnp.int32, (chunk, lanes), 0)
        token = (row // width) * PAGE
        low_flat = low.at[step].reshape(rows, lanes)
        high_flat = high.at[step].reshape(rows, lanes)
        code_flat = code.at[step].reshape(rows, lanes)

        def piece(c, carry):
            at = pl.ds(pl.multiple_of(c * chunk, chunk), chunk)
            left = limit - c * (chunk // width * PAGE)
            small = jnp.full((chunk, lanes), jnp.inf, jnp.float32)
            large = jnp.full((chunk, lanes), -jnp.inf, jnp.float32)
            total = jnp.zeros((chunk, lanes), jnp.float32)
            for t in range(PAGE):
                x = flat[t, at, :].astype(jnp.float32)
                keep = token < left - t
                small = jnp.where(keep, jnp.minimum(small, x), small)
                large = jnp.where(keep, jnp.maximum(large, x), large)
                total = jnp.where(keep, total + x, total)
            live = token < left
            small = jnp.where(live, small, 0.0)
            large = jnp.where(live, large, 0.0)
            bound = jnp.maximum(jnp.abs(small), jnp.abs(large))
            share = jnp.abs(total) / (PAGE * jnp.where(bound > 0.0, bound, 1.0))
            level = jnp.log2(jnp.maximum(share, 1e-30)) * (TOP / SPAN) + TOP
            level = jnp.clip(level + 0.5, 0.0, TOP)
            level = jnp.where(total < 0.0, -level, level)
            low_flat[at, :] = small.astype(low.dtype)
            high_flat[at, :] = large.astype(high.dtype)
            code_flat[at, :] = level.astype(jnp.int32).astype(jnp.int16)
            return carry

        lax.fori_loop(0, rows // chunk, piece, 0)
        itself = jnp.logical_and(mine, dest == seq)

        @pl.when(itself)
        def _():
            for k in range(3):
                local(step, k).start()

        @pl.when(jnp.logical_not(itself))
        def _():
            for k in range(3):
                remote(step, k).start()

        return carry

    lax.fori_loop(0, seqs, work, 0)

    for i in range(heads - 1):
        query_copy(i, lax.rem(head + i + 1, heads)).wait()
    own_query.wait()

    def finish(step, carry):
        itself = jnp.logical_and(mine, dest_of(step) == seq)

        @pl.when(itself)
        def _():
            for k in range(3):
                local(step, k).wait()

        @pl.when(jnp.logical_not(itself))
        def _():
            for k in range(3):
                remote(step, k).wait_send()

        return carry

    lax.fori_loop(0, seqs, finish, 0)

    def arrive(i, carry):
        source_head = i // ratio
        source_part = lax.rem(i, ratio)
        itself = jnp.logical_and(source_head == head, head * ratio + source_part == seq)

        @pl.when(jnp.logical_not(itself))
        def _():
            for k in range(3):
                source, target = trio[k]
                pltpu.make_async_remote_copy(
                    src_ref=source.at[0],
                    dst_ref=target.at[pl.ds(source_part * pages, pages), source_head],
                    send_sem=send_sem.at[0, k],
                    recv_sem=recv_sem.at[i, k],
                    device_id=(source_head, head * ratio + source_part),
                    device_id_type=MESH,
                ).wait_recv()

        return carry

    lax.fori_loop(0, seqs, arrive, 0)


def score_kernel(lengths, low, high, code, query, low_out, high_out, mean_out, score_out):
    block, kv_heads, lanes = low.shape
    count_q = query.shape[0]
    total_pages = block * pl.num_programs(0)
    start = lax.axis_index("head") * total_pages + pl.program_id(0) * block
    limit = lengths[lax.axis_index("seq")]
    small = low[...]
    large = high[...]
    low_out[0] = small
    high_out[0] = large
    bound = jnp.maximum(jnp.abs(small.astype(jnp.float32)), jnp.abs(large.astype(jnp.float32)))
    level = code[...].astype(jnp.int32).astype(jnp.float32)
    share = jnp.exp2((jnp.abs(level) - TOP) * (SPAN / TOP))
    total = jnp.where(level == 0.0, 0.0, share * (PAGE * bound))
    total = jnp.where(level < 0.0, -total, total)
    page = start + lax.broadcasted_iota(jnp.int32, (block, kv_heads, lanes), 0)
    count = jnp.clip(limit - page * PAGE, 1, PAGE).astype(jnp.float32)
    mean_out[0] = total / count
    q = query[...].astype(jnp.float32)
    positive = jnp.maximum(q, 0.0).astype(jnp.bfloat16)
    negative = jnp.minimum(q, 0.0).astype(jnp.bfloat16)
    dims = (((1,), (1,)), ((), ()))
    both = lax.dot_general(
        large.reshape(block * kv_heads, lanes), positive, dims, preferred_element_type=jnp.float32
    ) + lax.dot_general(
        small.reshape(block * kv_heads, lanes), negative, dims, preferred_element_type=jnp.float32
    )
    both = both.reshape(block, kv_heads, count_q)
    kv = lax.broadcasted_iota(jnp.int32, both.shape, 1)
    of = lax.broadcasted_iota(jnp.int32, both.shape, 2) // (count_q // kv_heads)
    score = jnp.sum(jnp.where(kv == of, both, 0.0), axis=1) * lanes ** (-0.5)
    score_out[0] = score.T


def local_step(heads, seqs, cached_keys, queries, seq_lengths):
    seq_count, tokens, width, lanes = cached_keys.shape
    pages = tokens // PAGE
    owned = pages * seqs // heads
    local_q = queries.shape[1]
    keys = cached_keys.reshape(seq_count, pages, PAGE, width, lanes)
    any_space = pl.BlockSpec(memory_space=pl.ANY)
    shape = (owned, heads, width, lanes)
    low, high, code, query = pl.pallas_call(
        functools.partial(page_kernel, seqs, heads),
        out_shape=(
            jax.ShapeDtypeStruct(shape, jnp.bfloat16),
            jax.ShapeDtypeStruct(shape, jnp.bfloat16),
            jax.ShapeDtypeStruct(shape, jnp.int16),
            jax.ShapeDtypeStruct((heads, local_q, lanes), jnp.bfloat16),
        ),
        in_specs=[pl.BlockSpec(memory_space=pltpu.SMEM), any_space, any_space],
        out_specs=(any_space,) * 4,
        scratch_shapes=[
            pltpu.VMEM((SLOTS, PAGE, pages, width, lanes), jnp.bfloat16),
            pltpu.VMEM((seqs, pages, width, lanes), jnp.bfloat16),
            pltpu.VMEM((seqs, pages, width, lanes), jnp.bfloat16),
            pltpu.VMEM((seqs, pages, width, lanes), jnp.int16),
            pltpu.SemaphoreType.DMA((SLOTS, PAGE)),
            pltpu.SemaphoreType.DMA((seqs, 3)),
            pltpu.SemaphoreType.DMA((seqs, 3)),
            pltpu.SemaphoreType.DMA((3,)),
            pltpu.SemaphoreType.DMA((heads - 1,)),
            pltpu.SemaphoreType.DMA((heads - 1,)),
            pltpu.SemaphoreType.DMA,
        ],
        compiler_params=pltpu.CompilerParams(collective_id=0, has_side_effects=True),
        name="page_exchange",
    )(seq_lengths, keys, queries.reshape(local_q, lanes))
    kv_heads = heads * width
    count_q = heads * local_q
    block = min(128, owned)
    page_spec = pl.BlockSpec((block, kv_heads, lanes), lambda i: (i, 0, 0))
    out_spec = pl.BlockSpec((1, block, kv_heads, lanes), lambda i: (0, i, 0, 0))
    whole = (1, owned, kv_heads, lanes)
    return pl.pallas_call(
        score_kernel,
        grid=(owned // block,),
        out_shape=(
            jax.ShapeDtypeStruct(whole, jnp.bfloat16),
            jax.ShapeDtypeStruct(whole, jnp.bfloat16),
            jax.ShapeDtypeStruct(whole, jnp.float32),
            jax.ShapeDtypeStruct((1, count_q, owned), jnp.float32),
        ),
        in_specs=[
            pl.BlockSpec(memory_space=pltpu.SMEM),
            page_spec,
            page_spec,
            page_spec,
            pl.BlockSpec((count_q, lanes), lambda i: (0, 0)),
        ],
        out_specs=(out_spec, out_spec, out_spec, pl.BlockSpec((1, count_q, block), lambda i: (0, 0, i))),
        name="page_score",
    )(
        seq_lengths,
        low.reshape(owned, kv_heads, lanes),
        high.reshape(owned, kv_heads, lanes),
        code.reshape(owned, kv_heads, lanes),
        query.reshape(count_q, lanes),
    )


def solution(mesh):
    return jax.shard_map(
        functools.partial(local_step, mesh.shape["head"], mesh.shape["seq"]),
        mesh=mesh,
        in_specs=(P(None, "seq", "head", None), P("seq", "head", None), P()),
        out_specs=(
            P("seq", "head", None, None),
            P("seq", "head", None, None),
            P("seq", "head", None, None),
            P("seq", None, "head"),
        ),
        check_vma=False,
    )
```

profile of v0, /device:TPU:19, one launch (start us, length us, event | category | flops | bytes accessed | tf_op | source)
XLA Modules:
  0.0 89.4 jit_solution(885410748543951286)
XLA Ops:
  0.6 82.7 %page_exchange.1 = (bf16[512,4,2,128]{3,2,1,0:T(2,128)(2,1)}, bf16[512,4,2,128]{3,2,1,0:T(2,128)(2,1)}, s16[512,4,2,128]{3,2,1,0:T(2,128)(2,1)}, bf16[4,16,128]{2,1,0:T(8,128)(2,1)}) custom-call(s32[8]{0:T(128)} %lengths.3, bf16[8,256,16,2,128]{4,3,2,1,0:T(2,128)(2,1)} %bitcast.6, bf16[16,128]{1,0:T(8,128)(2,1)} %bitcast.11), custom_call_target="tpu_custom_call" | custom-call | tf_op jit(solution)/shard_map/page_exchange/pallas_call | solution.py:238
  83.3 6.0 %page_score.1 = (bf16[1,512,8,128]{3,2,1,0:T(8,128)(2,1)}, bf16[1,512,8,128]{3,2,1,0:T(8,128)(2,1)}, f32[1,512,8,128]{3,2,1,0:T(8,128)}, f32[1,64,512]{2,1,0:T(8,128)}) custom-call(s32[8]{0:T(128)} %lengths.3, bf16[512,8,128]{2,1,0:T(8,128)(2,1)} %bitcast.7, bf16[512,8,128]{2,1,0:T(8,128)(2,1)} %bitcast.8, s16[512,8,128]{2,1,0:T(8,128)(2,1)} %bitcast.9, ...), custom_call_target="tpu_custom_call" | custom-call | tf_op jit(solution)/shard_map/page_score/pallas_call | solution.py:270
where the time goes:
time: 89.6 us; the launch traced here: 89.4 us
  Pallas kernels  88.7 us (99%)
    pallas_call x1, Pallas kernels, local_step(): pl.pallas_call(functools.partial(page_kernel, seqs, heads), out_shape=(ja...  82.7 us
    pallas_call x1, Pallas kernels, local_step(): pl.pallas_call(score_kernel, grid=(owned // block,), out_shape=(jax.Shape...  6.03 us

commit v1 on v0

v1 whole, which is shorter than its diff:
```python
import functools

import jax
import jax.numpy as jnp
from jax import lax
from jax.experimental import pallas as pl
from jax.experimental.pallas import tpu as pltpu
from jax.sharding import PartitionSpec as P

PAGE = 16
SLOTS = 3
BLOCK = 128
UNIT = 128
MESH = pl.DeviceIdType.MESH
SPAN = 28.0
TOP = 32767.0


def page_kernel(
    seqs, heads, lengths, keys, query, low_in, high_in, mean, score,
    buf, low, high, code, code_in, query_in, low_wide, high_wide, query_wide,
    key_sem, send_sem, recv_sem, query_send, query_recv, query_own,
):
    head = lax.axis_index("head")
    seq = lax.axis_index("seq")
    ratio = seqs // heads
    pages = keys.shape[1]
    width = keys.shape[3]
    lanes = keys.shape[4]
    block = buf.shape[2]
    blocks = pages // block
    steps = seqs * blocks
    rows = block * width
    chunk = min(64, rows)
    owner = seq // ratio
    part = lax.rem(seq, ratio)
    mine = owner == head

    def dest_of(step):
        pairs = seqs // 2
        half = pairs // 2
        k = step // blocks
        pair = k // 2
        own = seq // 2
        lower = own < half
        place = jnp.where(lower, own, pairs - 1 - own)
        near = jnp.where(place < half // 2, pairs - 1 - pair, pair - half)
        other = jnp.where(pair < half, pairs - 1 - pair, near)
        return 2 * jnp.where(lower, other, pairs - 1 - other) + lax.rem(seq + k, 2)

    def fetch(step):
        slot = lax.rem(step, SLOTS)
        dest = dest_of(step)
        at = pl.ds(lax.rem(step, blocks) * block, block)
        for t in range(PAGE):
            pltpu.make_async_copy(keys.at[dest, at, t], buf.at[slot, t], key_sem.at[slot]).start()

    for step in range(min(SLOTS - 1, steps)):
        fetch(jnp.int32(step))

    barrier = pltpu.get_barrier_semaphore()

    def greet(i, carry):
        source_head = i // ratio
        source_seq = head * ratio + lax.rem(i, ratio)

        @pl.when(jnp.logical_or(source_head != head, source_seq != seq))
        def _():
            pl.semaphore_signal(barrier, inc=1, device_id=(source_head, source_seq), device_id_type=MESH)

        return carry

    lax.fori_loop(0, seqs, greet, 0)
    for i in range(1, heads):
        pl.semaphore_signal(barrier, inc=1, device_id=(lax.rem(head + i, heads), seq), device_id_type=MESH)

    own_query = pltpu.make_async_copy(query, query_in.at[head], query_own)
    own_query.start()

    def query_copy(i, target):
        return pltpu.make_async_remote_copy(
            src_ref=query, dst_ref=query_in.at[head], send_sem=query_send.at[i], recv_sem=query_recv.at[i],
            device_id=(target, seq), device_id_type=MESH,
        )

    trio = ((low, low_in), (high, high_in), (code, code_in))
    index = head * ratio + part

    def landing(step):
        return pl.ds(part * pages + lax.rem(step, blocks) * block, block)

    def remote(step, k):
        source, target = trio[k]
        return pltpu.make_async_remote_copy(
            src_ref=source.at[step],
            dst_ref=target.at[landing(step), head],
            send_sem=send_sem.at[step, k],
            recv_sem=recv_sem.at[index, lax.rem(step, blocks), k],
            device_id=(owner, dest_of(step)),
            device_id_type=MESH,
        )

    row = lax.broadcasted_iota(jnp.int32, (chunk, lanes), 0)
    token = ((row // width) * PAGE).astype(jnp.int16)
    live_token = (row // width) * PAGE

    def work(step, carry):
        @pl.when(step + SLOTS - 1 < steps)
        def _():
            fetch(step + SLOTS - 1)

        slot = lax.rem(step, SLOTS)
        dest = dest_of(step)
        pltpu.make_async_copy(buf.at[slot], buf.at[slot], key_sem.at[slot]).wait()
        flat = buf.at[slot].reshape(PAGE, rows, lanes)
        limit = lengths[dest] - (seq * pages + lax.rem(step, blocks) * block) * PAGE
        low_flat = low.at[step].reshape(rows, lanes)
        high_flat = high.at[step].reshape(rows, lanes)
        code_flat = code.at[step].reshape(rows, lanes)

        def piece(c, carry):
            at = pl.ds(pl.multiple_of(c * chunk, chunk), chunk)
            left = jnp.clip(limit - c * (chunk // width * PAGE), 0, chunk // width * PAGE)
            first = flat[0, at, :]
            small = first
            large = first
            zero = jnp.zeros((chunk, lanes), jnp.bfloat16)
            total = jnp.where(token < left.astype(jnp.int16), first, zero).astype(jnp.float32)
            for t in range(1, PAGE):
                x = flat[t, at, :]
                keep = token < (left - t).astype(jnp.int16)
                y = jnp.where(keep, x, first)
                small = jnp.minimum(small, y)
                large = jnp.maximum(large, y)
                total = total + jnp.where(keep, x, zero).astype(jnp.float32)
            live = live_token < left
            small = jnp.where(live, small.astype(jnp.float32), 0.0)
            large = jnp.where(live, large.astype(jnp.float32), 0.0)
            bound = jnp.maximum(jnp.abs(small), jnp.abs(large))
            share = jnp.abs(total) / (PAGE * jnp.where(bound > 0.0, bound, 1.0))
            level = jnp.log2(jnp.maximum(share, 1e-30)) * (TOP / SPAN) + TOP
            level = jnp.clip(level + 0.5, 0.0, TOP)
            level = jnp.where(total < 0.0, -level, level)
            low_flat[at, :] = small.astype(low.dtype)
            high_flat[at, :] = large.astype(high.dtype)
            code_flat[at, :] = level.astype(jnp.int32).astype(jnp.int16)
            return carry

        lax.fori_loop(0, rows // chunk, piece, 0)

        @pl.when(step == 0)
        def _():
            pl.semaphore_wait(barrier, seqs - jnp.where(mine, 1, 0) + heads - 1)

        itself = jnp.logical_and(mine, dest == seq)

        @pl.when(itself)
        def _():
            low_in[landing(step), head] = low[step]
            high_in[landing(step), head] = high[step]
            code_in[landing(step), head] = code[step]

        @pl.when(jnp.logical_not(itself))
        def _():
            for k in range(3):
                remote(step, k).start()

        return carry

    lax.fori_loop(0, steps, work, 0)

    for i in range(heads - 1):
        query_copy(i, lax.rem(head + i + 1, heads)).start()
    own_query.wait()
    for i in range(heads - 1):
        query_copy(i, lax.rem(head + i + 1, heads)).wait()

    kv_heads = heads * width
    owned = mean.shape[0]
    group = query_in.shape[0] * query_in.shape[1] // kv_heads
    query_wide[...] = query_in[...].reshape(query_wide.shape).astype(jnp.float32)
    unit = min(UNIT, owned)
    unit_rows = unit * kv_heads
    span = max(pages // unit, 1)
    each = unit // block
    slab = min(128, unit_rows)
    limit = lengths[seq] - head * owned * PAGE
    low_flat = low_in.reshape(owned * kv_heads, lanes)
    high_flat = high_in.reshape(owned * kv_heads, lanes)
    code_flat = code_in.reshape(owned * kv_heads, lanes)
    mean_flat = mean.reshape(owned * kv_heads, lanes)
    page = lax.broadcasted_iota(jnp.int32, (slab, lanes), 0) // kv_heads

    def finish(i, carry):
        u = i
        if pages >= unit:
            u = lax.rem(i // span + seq, ratio) * span + lax.rem(i, span)

        def arrive(j, carry):
            source_head = j // each
            place = u * each + lax.rem(j, each)
            source_part = place // blocks
            itself = jnp.logical_and(source_head == head, head * ratio + source_part == seq)

            @pl.when(jnp.logical_not(itself))
            def _():
                for k in range(3):
                    source, target = trio[k]
                    pltpu.make_async_remote_copy(
                        src_ref=source.at[0],
                        dst_ref=target.at[pl.ds(place * block, block), source_head],
                        send_sem=send_sem.at[0, k],
                        recv_sem=recv_sem.at[source_head * ratio + source_part, lax.rem(place, blocks), k],
                        device_id=(source_head, head * ratio + source_part),
                        device_id_type=MESH,
                    ).wait_recv()

            return carry

        lax.fori_loop(0, heads * each, arrive, 0)

        def decode(c, carry):
            inside = pl.ds(pl.multiple_of(c * slab, slab), slab)
            at = pl.ds(pl.multiple_of(u * unit_rows + c * slab, slab), slab)
            small = low_flat[at, :].astype(jnp.float32)
            large = high_flat[at, :].astype(jnp.float32)
            low_wide[inside, :] = small
            high_wide[inside, :] = large
            bound = jnp.maximum(jnp.abs(small), jnp.abs(large))
            level = code_flat[at, :].astype(jnp.int32).astype(jnp.float32)
            share = jnp.exp2((jnp.abs(level) - TOP) * (SPAN / TOP))
            total = jnp.where(level == 0.0, 0.0, share * (PAGE * bound))
            total = jnp.where(level < 0.0, -total, total)
            first = u * unit + c * (slab // kv_heads)
            count = jnp.clip(limit - (first + page) * PAGE, 1, PAGE).astype(jnp.float32)
            mean_flat[at, :] = total / count
            return carry

        lax.fori_loop(0, unit_rows // slab, decode, 0)
        dims = (((1,), (1,)), ((), ()))
        across = pl.ds(pl.multiple_of(u * unit, unit), unit)
        for kv in range(kv_heads):
            q = query_wide[kv * group:(kv + 1) * group, :]
            up = high_wide[pl.ds(kv, unit, stride=kv_heads), :].astype(jnp.bfloat16)
            down = low_wide[pl.ds(kv, unit, stride=kv_heads), :].astype(jnp.bfloat16)
            both = lax.dot_general(
                jnp.maximum(q, 0.0).astype(jnp.bfloat16), up, dims, preferred_element_type=jnp.float32
            ) + lax.dot_general(
                jnp.minimum(q, 0.0).astype(jnp.bfloat16), down, dims, preferred_element_type=jnp.float32
            )
            score[kv * group:(kv + 1) * group, across] = both * lanes ** (-0.5)
        return carry

    lax.fori_loop(0, owned // unit, finish, 0)

    def sent(step, carry):
        @pl.when(jnp.logical_not(jnp.logical_and(mine, dest_of(step) == seq)))
        def _():
            for k in range(3):
                remote(step, k).wait_send()

        return carry

    lax.fori_loop(0, steps, sent, 0)


def store_kernel(low, high, mean, score, low_out, high_out, mean_out, score_out, sem):
    pairs = ((mean, mean_out), (low, low_out), (high, high_out), (score, score_out))
    copies = [pltpu.make_async_copy(source, target, sem.at[k]) for k, (source, target) in enumerate(pairs)]
    for copy in copies:
        copy.start()
    for copy in copies:
        copy.wait()


def local_step(heads, seqs, cached_keys, queries, seq_lengths):
    seq_count, tokens, width, lanes = cached_keys.shape
    pages = tokens // PAGE
    owned = pages * seqs // heads
    local_q = queries.shape[1]
    kv_heads = heads * width
    count_q = heads * local_q
    block = min(BLOCK, pages)
    blocks = pages // block
    unit = min(UNIT, owned)
    keys = cached_keys.reshape(seq_count, pages, PAGE, width, lanes)
    vmem = pl.BlockSpec(memory_space=pltpu.VMEM)
    hbm = pl.BlockSpec(memory_space=pltpu.HBM)
    shape = (owned, heads, width, lanes)
    low, high, mean, score = pl.pallas_call(
        functools.partial(page_kernel, seqs, heads),
        out_shape=(
            pltpu.VMEM(shape, jnp.bfloat16),
            pltpu.VMEM(shape, jnp.bfloat16),
            pltpu.VMEM((owned, kv_heads, lanes), jnp.float32),
            pltpu.VMEM((count_q, owned), jnp.float32),
        ),
        in_specs=[pl.BlockSpec(memory_space=pltpu.SMEM), hbm, hbm],
        out_specs=(vmem,) * 4,
        scratch_shapes=[
            pltpu.VMEM((SLOTS, PAGE, block, width, lanes), jnp.bfloat16),
            pltpu.VMEM((seqs * blocks, block, width, lanes), jnp.bfloat16),
            pltpu.VMEM((seqs * blocks, block, width, lanes), jnp.bfloat16),
            pltpu.VMEM((seqs * blocks, block, width, lanes), jnp.int16),
            pltpu.VMEM(shape, jnp.int16),
            pltpu.VMEM((heads, local_q, lanes), jnp.bfloat16),
            pltpu.VMEM((unit * kv_heads, lanes), jnp.float32),
            pltpu.VMEM((unit * kv_heads, lanes), jnp.float32),
            pltpu.VMEM((count_q, lanes), jnp.float32),
            pltpu.SemaphoreType.DMA((SLOTS,)),
            pltpu.SemaphoreType.DMA((seqs * blocks, 3)),
            pltpu.SemaphoreType.DMA((seqs, blocks, 3)),
            pltpu.SemaphoreType.DMA((heads - 1,)),
            pltpu.SemaphoreType.DMA((heads - 1,)),
            pltpu.SemaphoreType.DMA,
        ],
        compiler_params=pltpu.CompilerParams(collective_id=0, has_side_effects=True, vmem_limit_bytes=24 << 20),
        name="page_exchange",
    )(
        pltpu.with_memory_space_constraint(seq_lengths, pltpu.HBM),
        pltpu.with_memory_space_constraint(keys, pltpu.HBM),
        pltpu.with_memory_space_constraint(queries.reshape(local_q, lanes), pltpu.HBM),
    )
    whole = (1, owned, kv_heads, lanes)
    return pl.pallas_call(
        store_kernel,
        out_shape=(
            jax.ShapeDtypeStruct(whole, jnp.bfloat16),
            jax.ShapeDtypeStruct(whole, jnp.bfloat16),
            jax.ShapeDtypeStruct(whole, jnp.float32),
            jax.ShapeDtypeStruct((1, count_q, owned), jnp.float32),
        ),
        in_specs=[vmem] * 4,
        out_specs=(hbm,) * 4,
        scratch_shapes=[pltpu.SemaphoreType.DMA((4,))],
        compiler_params=pltpu.CompilerParams(vmem_limit_bytes=16 << 20),
        name="page_store",
    )(low.reshape(whole), high.reshape(whole), mean.reshape(whole), score.reshape(1, count_q, owned))


def solution(mesh):
    return jax.shard_map(
        functools.partial(local_step, mesh.shape["head"], mesh.shape["seq"]),
        mesh=mesh,
        in_specs=(P(None, "seq", "head", None), P("seq", "head", None), P()),
        out_specs=(
            P("seq", "head", None, None),
            P("seq", "head", None, None),
            P("seq", "head", None, None),
            P("seq", None, "head"),
        ),
        check_vma=False,
    )
```

time: 89.6 us -> 81.3 us (0.907); the launches traced: 89.4 us -> 80.1 us
  Pallas kernels: 88.7 us -> 79.4 us
    pallas_call x2, Pallas kernels: 88.7 us -> 79.4 us  [the longest x1 77.3 us: local_step(): pl.pallas_call(functools.partial(page_kernel, seqs, heads), out_shape=(pl...]
where the time goes in v1:
time: 81.3 us; the launch traced here: 80.1 us
  Pallas kernels  79.4 us (98%)
    pallas_call x1, Pallas kernels, local_step(): pl.pallas_call(functools.partial(page_kernel, seqs, heads), out_shape=(pl...  77.3 us
    pallas_call x1, Pallas kernels, local_step(): pl.pallas_call(store_kernel, out_shape=(jax.ShapeDtypeStruct(whole, jnp.b...  2.07 us

profile of v1, /device:TPU:19, one launch (start us, length us, event | category | flops | bytes accessed | tf_op | source)
XLA Modules:
  0.0 80.1 jit_solution(16180468622528614074)
XLA Ops:
  0.6 77.3 %page_exchange.1 = (bf16[512,4,2,128]{3,2,1,0:T(2,128)(2,1)S(1)}, bf16[512,4,2,128]{3,2,1,0:T(2,128)(2,1)S(1)}, f32[512,8,128]{2,1,0:T(8,128)S(1)}, f32[64,512]{1,0:T(8,128)S(1)}) custom-call(s32[8]{0:T(128)} %lengths.1, bf16[8,256,16,2,128]{4,3,2,1,0:T(2,128)(2,1)} %bitcast.10, bf16[16,128]{1,0:T(8,128)(2,1)} %bitcast.11), custom_call_target="tpu_custom_call" | custom-call | tf_op jit(solution)/shard_map/page_exchange/pallas_call | solution.py:290
  78.0 2.1 %page_store.1 = (bf16[1,512,8,128]{3,2,1,0:T(8,128)(2,1)}, bf16[1,512,8,128]{3,2,1,0:T(8,128)(2,1)}, f32[1,512,8,128]{3,2,1,0:T(8,128)}, f32[1,64,512]{2,1,0:T(8,128)}) custom-call(bf16[1,512,8,128]{3,2,1,0:T(8,128)(2,1)S(1)} %bitcast.7, bf16[1,512,8,128]{3,2,1,0:T(8,128)(2,1)S(1)} %bitcast.8, f32[1,512,8,128]{3,2,1,0:T(8,128)S(1)} %bitcast.6, ...), custom_call_target="tpu_custom_call" | custom-call | tf_op jit(solution)/shard_map/page_store/pallas_call | solution.py:325

commit v2 on v1

v2 whole, which is shorter than its diff:
```python
import functools

import jax
import jax.numpy as jnp
from jax import lax
from jax.experimental import pallas as pl
from jax.experimental.pallas import tpu as pltpu
from jax.sharding import PartitionSpec as P

PAGE = 16
SLOTS = 3
BLOCK = 128
UNIT = 128
MESH = pl.DeviceIdType.MESH
SPAN = 28.0
TOP = 32767.0


def gather(p, op, rows):
    early = rows < 4
    middle = jnp.logical_and(rows >= 2, rows < 6)
    even = lax.rem(rows, 4) < 2
    first = op(jnp.where(early, p[0], p[2]), pltpu.roll(jnp.where(early, p[2], p[0]), 4, 0))
    second = op(jnp.where(middle, p[1], p[3]), pltpu.roll(jnp.where(middle, p[3], p[1]), 4, 0))
    return op(jnp.where(even, first, second), pltpu.roll(jnp.where(even, second, first), 6, 0))


def shrink(x, op):
    x = op(x[:16], x[16:]).astype(jnp.float32)
    return op(x[:8], x[8:])


def page_kernel(
    seqs, heads, lengths_hbm, keys, query, low_in, high_in, mean, score,
    lengths, buf, low, high, code, code_in, query_in, low_wide, high_wide, query_wide,
    key_sem, send_sem, recv_sem, query_send, query_recv, query_own, length_sem,
):
    head = lax.axis_index("head")
    seq = lax.axis_index("seq")
    ratio = seqs // heads
    pages = keys.shape[1]
    tall = keys.shape[2]
    width = tall // PAGE
    lanes = keys.shape[3]
    block = buf.shape[1]
    blocks = pages // block
    steps = seqs * blocks
    rows = block * width
    group = min(8, block)
    chunk = min(32, block)
    owner = seq // ratio
    part = lax.rem(seq, ratio)
    mine = owner == head

    barrier = pltpu.get_barrier_semaphore()

    def greet(i, carry):
        source_head = i // ratio
        source_seq = head * ratio + lax.rem(i, ratio)

        @pl.when(jnp.logical_or(source_head != head, source_seq != seq))
        def _():
            pl.semaphore_signal(barrier, inc=1, device_id=(source_head, source_seq), device_id_type=MESH)

        return carry

    lax.fori_loop(0, seqs, greet, 0)
    for i in range(1, heads):
        pl.semaphore_signal(barrier, inc=1, device_id=(lax.rem(head + i, heads), seq), device_id_type=MESH)

    def dest_of(step):
        pairs = seqs // 2
        half = pairs // 2
        k = step // blocks
        pair = k // 2
        own = seq // 2
        lower = own < half
        place = jnp.where(lower, own, pairs - 1 - own)
        near = jnp.where(place < half // 2, pairs - 1 - pair, pair - half)
        other = jnp.where(pair < half, pairs - 1 - pair, near)
        return 2 * jnp.where(lower, other, pairs - 1 - other) + lax.rem(seq + k, 2)

    def fetch(step):
        slot = lax.rem(step, SLOTS)
        at = pl.ds(lax.rem(step, blocks) * block, block)
        return pltpu.make_async_copy(keys.at[dest_of(step), at], buf.at[slot], key_sem.at[slot])

    own_lengths = pltpu.make_async_copy(lengths_hbm, lengths, length_sem)
    own_lengths.start()
    for step in range(min(SLOTS - 1, steps)):
        fetch(jnp.int32(step)).start()
    own_query = pltpu.make_async_copy(query, query_in.at[head], query_own)
    own_query.start()

    def query_copy(i, target):
        return pltpu.make_async_remote_copy(
            src_ref=query, dst_ref=query_in.at[head], send_sem=query_send.at[i], recv_sem=query_recv.at[i],
            device_id=(target, seq), device_id_type=MESH,
        )

    trio = ((low, low_in), (high, high_in), (code, code_in))
    index = head * ratio + part

    def landing(step):
        return pl.ds(pl.multiple_of((part * pages + lax.rem(step, blocks) * block) * width, rows), rows)

    def remote(step, k):
        source, target = trio[k]
        return pltpu.make_async_remote_copy(
            src_ref=source.at[step],
            dst_ref=target.at[head, landing(step)],
            send_sem=send_sem.at[step, k],
            recv_sem=recv_sem.at[index, lax.rem(step, blocks), k],
            device_id=(owner, dest_of(step)),
            device_id_type=MESH,
        )

    adder_row = lax.broadcasted_iota(jnp.int32, (group * width, group * tall), 0)
    adder_column = lax.broadcasted_iota(jnp.int32, (group * width, group * tall), 1)
    adder = jnp.logical_and(
        adder_row // width == adder_column // tall, lax.rem(adder_row, width) == lax.rem(adder_column, width)
    ).astype(jnp.bfloat16)
    adder_token = (adder_column // width).astype(jnp.int16)
    eight = lax.broadcasted_iota(jnp.int32, (8, lanes), 0)
    page_of = lax.broadcasted_iota(jnp.int32, (chunk * width, lanes), 0) // width
    token_of = (lax.broadcasted_iota(jnp.int32, (tall, lanes), 0) // width).astype(jnp.int16)
    above = jnp.full((tall, lanes), jnp.inf, jnp.bfloat16)
    own_lengths.wait()

    def work(step, carry):
        @pl.when(step + SLOTS - 1 < steps)
        def _():
            fetch(step + SLOTS - 1).start()

        slot = lax.rem(step, SLOTS)
        dest = dest_of(step)
        fetch(step).wait()
        limit = jnp.clip(lengths[dest] - (seq * pages + lax.rem(step, blocks) * block) * PAGE, 0, block * PAGE)

        def piece(c, carry):
            small, large, total = [], [], []
            for g in range(chunk // group):
                start = c * chunk + g * group
                left = limit - start * PAGE
                lows, highs = [], []
                for p in range(group):
                    x = buf[slot, start + p]
                    keep = token_of < jnp.clip(left - p * PAGE, 0, PAGE).astype(jnp.int16)
                    lows.append(shrink(jnp.where(keep, x, above), jnp.minimum))
                    highs.append(shrink(jnp.where(keep, x, -above), jnp.maximum))
                for p in range(0, group, 4):
                    small.append(gather(lows[p:p + 4], jnp.minimum, eight))
                    large.append(gather(highs[p:p + 4], jnp.maximum, eight))
                x = buf[slot, pl.ds(start, group)].reshape(group * tall, lanes)
                counted = adder_token < jnp.clip(left, 0, group * PAGE).astype(jnp.int16)
                weight = jnp.where(counted, adder, jnp.zeros_like(adder))
                total.append(jnp.dot(weight, x, preferred_element_type=jnp.float32))
            live = (page_of + c * chunk) * PAGE < limit
            small = jnp.where(live, jnp.concatenate(small, axis=0), 0.0)
            large = jnp.where(live, jnp.concatenate(large, axis=0), 0.0)
            total = jnp.concatenate(total, axis=0)
            bound = jnp.maximum(jnp.abs(small), jnp.abs(large))
            share = jnp.abs(total) / (PAGE * jnp.where(bound > 0.0, bound, 1.0))
            level = jnp.log2(jnp.maximum(share, 1e-30)) * (TOP / SPAN) + TOP
            level = jnp.clip(level + 0.5, 0.0, TOP)
            level = jnp.where(total < 0.0, -level, level)
            at = pl.ds(pl.multiple_of(c * chunk * width, chunk * width), chunk * width)
            low[step, at, :] = small.astype(low.dtype)
            high[step, at, :] = large.astype(high.dtype)
            code[step, at, :] = level.astype(jnp.int32).astype(jnp.int16)
            return carry

        lax.fori_loop(0, block // chunk, piece, 0)

        @pl.when(step == 0)
        def _():
            pl.semaphore_wait(barrier, seqs - jnp.where(mine, 1, 0) + heads - 1)

        itself = jnp.logical_and(mine, dest == seq)

        @pl.when(itself)
        def _():
            low_in[head, landing(step)] = low[step]
            high_in[head, landing(step)] = high[step]
            code_in[head, landing(step)] = code[step]

        @pl.when(jnp.logical_not(itself))
        def _():
            for k in range(3):
                remote(step, k).start()

        return carry

    lax.fori_loop(0, steps, work, 0)

    for i in range(heads - 1):
        query_copy(i, lax.rem(head + i + 1, heads)).start()
    own_query.wait()
    for i in range(heads - 1):
        query_copy(i, lax.rem(head + i + 1, heads)).wait()

    owned = pages * ratio
    shared = query_in.shape[1] // width
    query_wide[...] = query_in[...].reshape(query_wide.shape).astype(jnp.float32)
    unit = min(UNIT, owned)
    unit_rows = unit * width
    span = max(pages // unit, 1)
    each = unit // block
    slab = min(128, unit_rows)
    limit = lengths[seq] - head * owned * PAGE
    row_page = lax.broadcasted_iota(jnp.int32, (slab, lanes), 0) // width

    def finish(i, carry):
        u = i // heads
        source_head = lax.rem(i, heads)
        if pages >= unit:
            u = lax.rem(u // span + seq, ratio) * span + lax.rem(u, span)

        def arrive(j, carry):
            place = u * each + j
            source_part = place // blocks
            itself = jnp.logical_and(source_head == head, head * ratio + source_part == seq)

            @pl.when(jnp.logical_not(itself))
            def _():
                for k in range(3):
                    source, target = trio[k]
                    pltpu.make_async_remote_copy(
                        src_ref=source.at[0],
                        dst_ref=target.at[source_head, pl.ds(pl.multiple_of(place * rows, rows), rows)],
                        send_sem=send_sem.at[0, k],
                        recv_sem=recv_sem.at[source_head * ratio + source_part, lax.rem(place, blocks), k],
                        device_id=(source_head, head * ratio + source_part),
                        device_id_type=MESH,
                    ).wait_recv()

            return carry

        lax.fori_loop(0, each, arrive, 0)

        def decode(c, carry):
            inside = pl.ds(pl.multiple_of(c * slab, slab), slab)
            at = pl.ds(pl.multiple_of(u * unit_rows + c * slab, slab), slab)
            small = low_in[source_head, at, :].astype(jnp.float32)
            large = high_in[source_head, at, :].astype(jnp.float32)
            low_wide[inside, :] = small
            high_wide[inside, :] = large
            bound = jnp.maximum(jnp.abs(small), jnp.abs(large))
            level = code_in[source_head, at, :].astype(jnp.int32).astype(jnp.float32)
            share = jnp.exp2((jnp.abs(level) - TOP) * (SPAN / TOP))
            total = jnp.where(level == 0.0, 0.0, share * (PAGE * bound))
            total = jnp.where(level < 0.0, -total, total)
            first = u * unit + c * (slab // width)
            count = jnp.clip(limit - (first + row_page) * PAGE, 1, PAGE).astype(jnp.float32)
            mean[source_head, at, :] = total / count
            return carry

        lax.fori_loop(0, unit_rows // slab, decode, 0)
        dims = (((1,), (1,)), ((), ()))
        across = pl.ds(pl.multiple_of(u * unit, unit), unit)
        for j in range(width):
            at = pl.ds(pl.multiple_of((source_head * width + j) * shared, shared), shared)
            q = query_wide[at, :]
            up = high_wide[pl.ds(j, unit, stride=width), :].astype(jnp.bfloat16)
            down = low_wide[pl.ds(j, unit, stride=width), :].astype(jnp.bfloat16)
            both = lax.dot_general(
                jnp.maximum(q, 0.0).astype(jnp.bfloat16), up, dims, preferred_element_type=jnp.float32
            ) + lax.dot_general(
                jnp.minimum(q, 0.0).astype(jnp.bfloat16), down, dims, preferred_element_type=jnp.float32
            )
            score[at, across] = both * lanes ** (-0.5)
        return carry

    lax.fori_loop(0, owned // unit * heads, finish, 0)

    def sent(step, carry):
        @pl.when(jnp.logical_not(jnp.logical_and(mine, dest_of(step) == seq)))
        def _():
            for k in range(3):
                remote(step, k).wait_send()

        return carry

    lax.fori_loop(0, steps, sent, 0)


def store_kernel(low, high, mean, score, low_out, high_out, mean_out, score_out, sem):
    heads = low.shape[0]
    copies = []
    for k, (source, target) in enumerate(((mean, mean_out), (low, low_out), (high, high_out))):
        for head in range(heads):
            copies.append(pltpu.make_async_copy(source.at[head], target.at[:, head], sem.at[k, head]))
    copies.append(pltpu.make_async_copy(score, score_out, sem.at[3, 0]))
    for copy in copies:
        copy.start()
    for copy in copies:
        copy.wait()


def local_step(heads, seqs, cached_keys, queries, seq_lengths):
    seq_count, tokens, width, lanes = cached_keys.shape
    pages = tokens // PAGE
    owned = pages * seqs // heads
    local_q = queries.shape[1]
    kv_heads = heads * width
    count_q = heads * local_q
    block = min(BLOCK, pages)
    blocks = pages // block
    unit = min(UNIT, owned)
    tall = PAGE * width
    keys = cached_keys.reshape(seq_count, pages, tall, lanes)
    vmem = pl.BlockSpec(memory_space=pltpu.VMEM)
    hbm = pl.BlockSpec(memory_space=pltpu.HBM)
    shape = (heads, owned * width, lanes)
    sends = (seqs * blocks, block * width, lanes)
    low, high, mean, score = pl.pallas_call(
        functools.partial(page_kernel, seqs, heads),
        out_shape=(
            pltpu.VMEM(shape, jnp.bfloat16),
            pltpu.VMEM(shape, jnp.bfloat16),
            pltpu.VMEM(shape, jnp.float32),
            pltpu.VMEM((count_q, owned), jnp.float32),
        ),
        in_specs=[hbm] * 3,
        out_specs=(vmem,) * 4,
        scratch_shapes=[
            pltpu.SMEM((seq_count,), jnp.int32),
            pltpu.VMEM((SLOTS, block, tall, lanes), jnp.bfloat16),
            pltpu.VMEM(sends, jnp.bfloat16),
            pltpu.VMEM(sends, jnp.bfloat16),
            pltpu.VMEM(sends, jnp.int16),
            pltpu.VMEM(shape, jnp.int16),
            pltpu.VMEM((heads, local_q, lanes), jnp.bfloat16),
            pltpu.VMEM((unit * width, lanes), jnp.float32),
            pltpu.VMEM((unit * width, lanes), jnp.float32),
            pltpu.VMEM((count_q, lanes), jnp.float32),
            pltpu.SemaphoreType.DMA((SLOTS,)),
            pltpu.SemaphoreType.DMA((seqs * blocks, 3)),
            pltpu.SemaphoreType.DMA((seqs, blocks, 3)),
            pltpu.SemaphoreType.DMA((heads - 1,)),
            pltpu.SemaphoreType.DMA((heads - 1,)),
            pltpu.SemaphoreType.DMA,
            pltpu.SemaphoreType.DMA,
        ],
        compiler_params=pltpu.CompilerParams(collective_id=0, has_side_effects=True, vmem_limit_bytes=24 << 20),
        name="page_exchange",
    )(
        pltpu.with_memory_space_constraint(seq_lengths, pltpu.HBM),
        pltpu.with_memory_space_constraint(keys, pltpu.HBM),
        pltpu.with_memory_space_constraint(queries.reshape(local_q, lanes), pltpu.HBM),
    )
    split = (heads, owned, width, lanes)
    whole = (owned, heads, width, lanes)
    low, high, mean, score = pl.pallas_call(
        store_kernel,
        out_shape=(
            jax.ShapeDtypeStruct(whole, jnp.bfloat16),
            jax.ShapeDtypeStruct(whole, jnp.bfloat16),
            jax.ShapeDtypeStruct(whole, jnp.float32),
            jax.ShapeDtypeStruct((count_q, owned), jnp.float32),
        ),
        in_specs=[vmem] * 4,
        out_specs=(hbm,) * 4,
        scratch_shapes=[pltpu.SemaphoreType.DMA((4, heads))],
        compiler_params=pltpu.CompilerParams(vmem_limit_bytes=16 << 20),
        name="page_store",
    )(low.reshape(split), high.reshape(split), mean.reshape(split), score)
    final = (1, owned, kv_heads, lanes)
    return low.reshape(final), high.reshape(final), mean.reshape(final), score.reshape(1, count_q, owned)


def solution(mesh):
    return jax.shard_map(
        functools.partial(local_step, mesh.shape["head"], mesh.shape["seq"]),
        mesh=mesh,
        in_specs=(P(None, "seq", "head", None), P("seq", "head", None), P()),
        out_specs=(
            P("seq", "head", None, None),
            P("seq", "head", None, None),
            P("seq", "head", None, None),
            P("seq", None, "head"),
        ),
        check_vma=False,
    )
```

time: 81.3 us -> 79.1 us (0.973)
  Pallas kernels: 79.4 us -> 77 us
    pallas_call x1, Pallas kernels: 77.3 us -> 74.9 us  [local_step(): pl.pallas_call(functools.partial(page_kernel, seqs, heads), out_shape=(pl...]
where the time goes in v2:
time: 79.1 us; the launch traced here: 77.7 us
  Pallas kernels  77 us (97%)
    pallas_call x1, Pallas kernels, local_step(): pl.pallas_call(functools.partial(page_kernel, seqs, heads), out_shape=(pl...  74.9 us
    pallas_call x1, Pallas kernels, local_step(): pl.pallas_call(store_kernel, out_shape=(jax.ShapeDtypeStruct(whole, jnp.b...  2.18 us

profile of v2, /device:TPU:19, one launch (start us, length us, event | category | flops | bytes accessed | tf_op | source)
XLA Modules:
  0.0 77.7 jit_solution(11117617897015623895)
XLA Ops:
  0.6 74.9 %page_exchange.1 = (bf16[4,1024,128]{2,1,0:T(8,128)(2,1)S(1)}, bf16[4,1024,128]{2,1,0:T(8,128)(2,1)S(1)}, f32[4,1024,128]{2,1,0:T(8,128)S(1)}, f32[64,512]{1,0:T(8,128)S(1)}) custom-call(s32[8]{0:T(128)} %lengths_hbm.1, bf16[8,256,32,128]{3,2,1,0:T(8,128)(2,1)} %bitcast.12, bf16[16,128]{1,0:T(8,128)(2,1)} %bitcast.13), custom_call_target="tpu_custom_call" | custom-call | tf_op jit(solution)/shard_map/page_exchange/pallas_call | solution.py:316
  75.5 2.2 %page_store.1 = (bf16[512,4,2,128]{3,2,1,0:T(2,128)(2,1)}, bf16[512,4,2,128]{3,2,1,0:T(2,128)(2,1)}, f32[512,4,2,128]{3,2,1,0:T(2,128)}, f32[64,512]{1,0:T(8,128)}) custom-call(bf16[4,512,2,128]{3,2,1,0:T(2,128)(2,1)S(1)} %bitcast.10, bf16[4,512,2,128]{3,2,1,0:T(2,128)(2,1)S(1)} %bitcast.11, f32[4,512,2,128]{3,2,1,0:T(2,128)S(1)} %bitcast.9, ...), custom_call_target="tpu_custom_call" | custom-call | tf_op jit(solution)/shard_map/page_store/pallas_call | solution.py:354

commit v3 on v2

--- a/solution.py
+++ b/solution.py
@@ -210,12 +210,9 @@
     limit = lengths[seq] - head * owned * PAGE
     row_page = lax.broadcasted_iota(jnp.int32, (slab, lanes), 0) // width
 
-    def finish(i, carry):
-        u = i // heads
-        source_head = lax.rem(i, heads)
-        if pages >= unit:
-            u = lax.rem(u // span + seq, ratio) * span + lax.rem(u, span)
-
+    dims = (((1,), (1,)), ((), ()))
+
+    def arrived(u, source_head, kinds):
         def arrive(j, carry):
             place = u * each + j
             source_part = place // blocks
@@ -223,7 +220,7 @@
 
             @pl.when(jnp.logical_not(itself))
             def _():
-                for k in range(3):
+                for k in kinds:
                     source, target = trio[k]
                     pltpu.make_async_remote_copy(
                         src_ref=source.at[0],
@@ -238,40 +235,63 @@
 
         lax.fori_loop(0, each, arrive, 0)
 
-        def decode(c, carry):
-            inside = pl.ds(pl.multiple_of(c * slab, slab), slab)
-            at = pl.ds(pl.multiple_of(u * unit_rows + c * slab, slab), slab)
-            small = low_in[source_head, at, :].astype(jnp.float32)
-            large = high_in[source_head, at, :].astype(jnp.float32)
-            low_wide[inside, :] = small
-            high_wide[inside, :] = large
-            bound = jnp.maximum(jnp.abs(small), jnp.abs(large))
-            level = code_in[source_head, at, :].astype(jnp.int32).astype(jnp.float32)
-            share = jnp.exp2((jnp.abs(level) - TOP) * (SPAN / TOP))
-            total = jnp.where(level == 0.0, 0.0, share * (PAGE * bound))
-            total = jnp.where(level < 0.0, -total, total)
-            first = u * unit + c * (slab // width)
-            count = jnp.clip(limit - (first + row_page) * PAGE, 1, PAGE).astype(jnp.float32)
-            mean[source_head, at, :] = total / count
+    def finish(i, carry):
+        u = i
+        if pages >= unit:
+            u = lax.rem(i // span + seq, ratio) * span + lax.rem(i, span)
+        across = pl.ds(pl.multiple_of(u * unit, unit), unit)
+
+        def place_of(c):
+            return pl.ds(pl.multiple_of(u * unit_rows + c * slab, slab), slab)
+
+        def bounds(source_head, carry):
+            arrived(u, source_head, (0, 1))
+
+            def widen(c, carry):
+                inside = pl.ds(pl.multiple_of(c * slab, slab), slab)
+                at = place_of(c)
+                small = low_in[source_head, at, :].astype(jnp.float32)
+                large = high_in[source_head, at, :].astype(jnp.float32)
+                low_wide[inside, :] = small
+                high_wide[inside, :] = large
+                first = u * unit + c * (slab // width)
+                count = jnp.clip(limit - (first + row_page) * PAGE, 1, PAGE).astype(jnp.float32)
+                mean[source_head, at, :] = jnp.maximum(jnp.abs(small), jnp.abs(large)) * PAGE / count
+                return carry
+
+            lax.fori_loop(0, unit_rows // slab, widen, 0)
+            for j in range(width):
+                at = pl.ds(pl.multiple_of((source_head * width + j) * shared, shared), shared)
+                q = query_wide[at, :]
+                up = high_wide[pl.ds(j, unit, stride=width), :].astype(jnp.bfloat16)
+                down = low_wide[pl.ds(j, unit, stride=width), :].astype(jnp.bfloat16)
+                both = lax.dot_general(
+                    jnp.maximum(q, 0.0).astype(jnp.bfloat16), up, dims, preferred_element_type=jnp.float32
+                ) + lax.dot_general(
+                    jnp.minimum(q, 0.0).astype(jnp.bfloat16), down, dims, preferred_element_type=jnp.float32
+                )
+                score[at, across] = both * lanes ** (-0.5)
             return carry
 
-        lax.fori_loop(0, unit_rows // slab, decode, 0)
-        dims = (((1,), (1,)), ((), ()))
-        across = pl.ds(pl.multiple_of(u * unit, unit), unit)
-        for j in range(width):
-            at = pl.ds(pl.multiple_of((source_head * width + j) * shared, shared), shared)
-            q = query_wide[at, :]
-            up = high_wide[pl.ds(j, unit, stride=width), :].astype(jnp.bfloat16)
-            down = low_wide[pl.ds(j, unit, stride=width), :].astype(jnp.bfloat16)
-            both = lax.dot_general(
-                jnp.maximum(q, 0.0).astype(jnp.bfloat16), up, dims, preferred_element_type=jnp.float32
-            ) + lax.dot_general(
-                jnp.minimum(q, 0.0).astype(jnp.bfloat16), down, dims, preferred_element_type=jnp.float32
-            )
-            score[at, across] = both * lanes ** (-0.5)
+        def means(source_head, carry):
+            arrived(u, source_head, (2,))
+
+            def decode(c, carry):
+                at = place_of(c)
+                level = code_in[source_head, at, :].astype(jnp.int32).astype(jnp.float32)
+                share = jnp.exp2((jnp.abs(level) - TOP) * (SPAN / TOP))
+                share = jnp.where(level == 0.0, 0.0, jnp.where(level < 0.0, -share, share))
+                mean[source_head, at, :] = mean[source_head, at, :] * share
+                return carry
+
+            lax.fori_loop(0, unit_rows // slab, decode, 0)
+            return carry
+
+        lax.fori_loop(0, heads, bounds, 0)
+        lax.fori_loop(0, heads, means, 0)
         return carry
 
-    lax.fori_loop(0, owned // unit * heads, finish, 0)
+    lax.fori_loop(0, owned // unit, finish, 0)
 
     def sent(step, carry):
         @pl.when(jnp.logical_not(jnp.logical_and(mine, dest_of(step) == seq)))

time: 79.1 us -> 78.2 us (0.989)
  no operation moved by 1% of the time
where the time goes in v3:
time: 78.2 us; the launch traced here: 77.3 us
  Pallas kernels  76.6 us (98%)
    pallas_call x1, Pallas kernels, local_step(): pl.pallas_call(functools.partial(page_kernel, seqs, heads), out_shape=(pl...  74.5 us
    pallas_call x1, Pallas kernels, local_step(): pl.pallas_call(store_kernel, out_shape=(jax.ShapeDtypeStruct(whole, jnp.b...  2.18 us

profile of v3, /device:TPU:19, one launch (start us, length us, event | category | flops | bytes accessed | tf_op | source)
XLA Modules:
  0.0 77.3 jit_solution(10843246129525908152)
XLA Ops:
  0.6 74.5 %page_exchange.1 = (bf16[4,1024,128]{2,1,0:T(8,128)(2,1)S(1)}, bf16[4,1024,128]{2,1,0:T(8,128)(2,1)S(1)}, f32[4,1024,128]{2,1,0:T(8,128)S(1)}, f32[64,512]{1,0:T(8,128)S(1)}) custom-call(s32[8]{0:T(128)} %lengths_hbm.1, bf16[8,256,32,128]{3,2,1,0:T(8,128)(2,1)} %bitcast.12, bf16[16,128]{1,0:T(8,128)(2,1)} %bitcast.13), custom_call_target="tpu_custom_call" | custom-call | tf_op jit(solution)/shard_map/page_exchange/pallas_call | solution.py:336
  75.1 2.2 %page_store.1 = (bf16[512,4,2,128]{3,2,1,0:T(2,128)(2,1)}, bf16[512,4,2,128]{3,2,1,0:T(2,128)(2,1)}, f32[512,4,2,128]{3,2,1,0:T(2,128)}, f32[64,512]{1,0:T(8,128)}) custom-call(bf16[4,512,2,128]{3,2,1,0:T(2,128)(2,1)S(1)} %bitcast.10, bf16[4,512,2,128]{3,2,1,0:T(2,128)(2,1)S(1)} %bitcast.11, f32[4,512,2,128]{3,2,1,0:T(2,128)S(1)} %bitcast.9, ...), custom_call_target="tpu_custom_call" | custom-call | tf_op jit(solution)/shard_map/page_store/pallas_call | solution.py:374

commit v4 on v3

--- a/solution.py
+++ b/solution.py
@@ -10,7 +10,7 @@
 PAGE = 16
 SLOTS = 3
 BLOCK = 128
-UNIT = 128
+LANE = 128
 MESH = pl.DeviceIdType.MESH
 SPAN = 28.0
 TOP = 32767.0
@@ -31,9 +31,9 @@
 
 
 def page_kernel(
-    seqs, heads, lengths_hbm, keys, query, low_in, high_in, mean, score,
-    lengths, buf, low, high, code, code_in, query_in, low_wide, high_wide, query_wide,
-    key_sem, send_sem, recv_sem, query_send, query_recv, query_own, length_sem,
+    seqs, heads, lengths_hbm, keys, query, bounds_in, mean, score,
+    lengths, buf, bounds, code, code_in, query_in, low_wide, high_wide, query_wide,
+    key_sem, bounds_send, bounds_recv, code_send, code_recv, query_send, query_recv, query_own, length_sem,
 ):
     head = lax.axis_index("head")
     seq = lax.axis_index("seq")
@@ -98,19 +98,40 @@
             device_id=(target, seq), device_id_type=MESH,
         )
 
-    trio = ((low, low_in), (high, high_in), (code, code_in))
     index = head * ratio + part
 
     def landing(step):
         return pl.ds(pl.multiple_of((part * pages + lax.rem(step, blocks) * block) * width, rows), rows)
 
-    def remote(step, k):
-        source, target = trio[k]
+    def inside_of(step):
+        return pl.ds(pl.multiple_of(lax.rem(step, blocks) * rows, rows), rows)
+
+    def whole_bounds(step):
         return pltpu.make_async_remote_copy(
-            src_ref=source.at[step],
-            dst_ref=target.at[head, landing(step)],
-            send_sem=send_sem.at[step, k],
-            recv_sem=recv_sem.at[index, lax.rem(step, blocks), k],
+            src_ref=bounds.at[step // blocks],
+            dst_ref=bounds_in.at[head, part],
+            send_sem=bounds_send.at[step // blocks],
+            recv_sem=bounds_recv.at[index],
+            device_id=(owner, dest_of(step)),
+            device_id_type=MESH,
+        )
+
+    def block_bounds(step):
+        return pltpu.make_async_remote_copy(
+            src_ref=bounds.at[step // blocks, :, inside_of(step)],
+            dst_ref=bounds_in.at[head, part, :, inside_of(step)],
+            send_sem=bounds_send.at[step // blocks],
+            recv_sem=bounds_recv.at[index],
+            device_id=(owner, dest_of(step)),
+            device_id_type=MESH,
+        )
+
+    def block_code(step):
+        return pltpu.make_async_remote_copy(
+            src_ref=code.at[step // blocks, inside_of(step)],
+            dst_ref=code_in.at[head, landing(step)],
+            send_sem=code_send.at[step],
+            recv_sem=code_recv.at[index, lax.rem(step, blocks)],
             device_id=(owner, dest_of(step)),
             device_id_type=MESH,
         )
@@ -164,10 +185,10 @@
             level = jnp.log2(jnp.maximum(share, 1e-30)) * (TOP / SPAN) + TOP
             level = jnp.clip(level + 0.5, 0.0, TOP)
             level = jnp.where(total < 0.0, -level, level)
-            at = pl.ds(pl.multiple_of(c * chunk * width, chunk * width), chunk * width)
-            low[step, at, :] = small.astype(low.dtype)
-            high[step, at, :] = large.astype(high.dtype)
-            code[step, at, :] = level.astype(jnp.int32).astype(jnp.int16)
+            at = pl.ds(pl.multiple_of(lax.rem(step, blocks) * rows + c * chunk * width, chunk * width), chunk * width)
+            bounds[step // blocks, 0, at, :] = small.astype(bounds.dtype)
+            bounds[step // blocks, 1, at, :] = large.astype(bounds.dtype)
+            code[step // blocks, at, :] = level.astype(jnp.int32).astype(jnp.int16)
             return carry
 
         lax.fori_loop(0, block // chunk, piece, 0)
@@ -180,14 +201,21 @@
 
         @pl.when(itself)
         def _():
-            low_in[head, landing(step)] = low[step]
-            high_in[head, landing(step)] = high[step]
-            code_in[head, landing(step)] = code[step]
-
-        @pl.when(jnp.logical_not(itself))
-        def _():
-            for k in range(3):
-                remote(step, k).start()
+            bounds_in[head, part, :, inside_of(step)] = bounds[step // blocks, :, inside_of(step)]
+            code_in[head, landing(step)] = code[step // blocks, inside_of(step)]
+
+        @pl.when(jnp.logical_and(jnp.logical_not(itself), step < blocks))
+        def _():
+            block_bounds(step).start()
+            block_code(step).start()
+
+        complete = jnp.logical_and(step >= blocks, lax.rem(step, blocks) == blocks - 1)
+
+        @pl.when(jnp.logical_and(jnp.logical_not(itself), complete))
+        def _():
+            whole_bounds(step).start()
+            for b in range(blocks):
+                block_code(step - (blocks - 1) + b).start()
 
         return carry
 
@@ -202,56 +230,47 @@
     owned = pages * ratio
     shared = query_in.shape[1] // width
     query_wide[...] = query_in[...].reshape(query_wide.shape).astype(jnp.float32)
-    unit = min(UNIT, owned)
+    unit = min(max(LANE, pages), owned)
     unit_rows = unit * width
-    span = max(pages // unit, 1)
-    each = unit // block
-    slab = min(128, unit_rows)
+    each = unit // pages
+    message = pages * width
+    slab = min(256, rows)
+    parts = message // slab
     limit = lengths[seq] - head * owned * PAGE
     row_page = lax.broadcasted_iota(jnp.int32, (slab, lanes), 0) // width
 
     dims = (((1,), (1,)), ((), ()))
 
-    def arrived(u, source_head, kinds):
-        def arrive(j, carry):
-            place = u * each + j
-            source_part = place // blocks
-            itself = jnp.logical_and(source_head == head, head * ratio + source_part == seq)
-
-            @pl.when(jnp.logical_not(itself))
-            def _():
-                for k in kinds:
-                    source, target = trio[k]
+    def finish(i, carry):
+        u = i
+        if each == 1:
+            u = lax.rem(i + seq, ratio)
+        across = pl.ds(pl.multiple_of(u * unit, unit), unit)
+
+        def elsewhere(source_head, source_part):
+            return jnp.logical_or(source_head != head, head * ratio + source_part != seq)
+
+        def spread(source_head, carry):
+            for j in range(each):
+                source_part = u * each + j
+
+                @pl.when(elsewhere(source_head, source_part))
+                def _():
                     pltpu.make_async_remote_copy(
-                        src_ref=source.at[0],
-                        dst_ref=target.at[source_head, pl.ds(pl.multiple_of(place * rows, rows), rows)],
-                        send_sem=send_sem.at[0, k],
-                        recv_sem=recv_sem.at[source_head * ratio + source_part, lax.rem(place, blocks), k],
+                        src_ref=bounds.at[0],
+                        dst_ref=bounds_in.at[source_head, source_part],
+                        send_sem=bounds_send.at[0],
+                        recv_sem=bounds_recv.at[source_head * ratio + source_part],
                         device_id=(source_head, head * ratio + source_part),
                         device_id_type=MESH,
                     ).wait_recv()
 
-            return carry
-
-        lax.fori_loop(0, each, arrive, 0)
-
-    def finish(i, carry):
-        u = i
-        if pages >= unit:
-            u = lax.rem(i // span + seq, ratio) * span + lax.rem(i, span)
-        across = pl.ds(pl.multiple_of(u * unit, unit), unit)
-
-        def place_of(c):
-            return pl.ds(pl.multiple_of(u * unit_rows + c * slab, slab), slab)
-
-        def bounds(source_head, carry):
-            arrived(u, source_head, (0, 1))
-
             def widen(c, carry):
                 inside = pl.ds(pl.multiple_of(c * slab, slab), slab)
-                at = place_of(c)
-                small = low_in[source_head, at, :].astype(jnp.float32)
-                large = high_in[source_head, at, :].astype(jnp.float32)
+                at = pl.ds(pl.multiple_of(u * unit_rows + c * slab, slab), slab)
+                local = pl.ds(pl.multiple_of(lax.rem(c, parts) * slab, slab), slab)
+                small = bounds_in[source_head, u * each + c // parts, 0, local, :].astype(jnp.float32)
+                large = bounds_in[source_head, u * each + c // parts, 1, local, :].astype(jnp.float32)
                 low_wide[inside, :] = small
                 high_wide[inside, :] = large
                 first = u * unit + c * (slab // width)
@@ -273,22 +292,35 @@
                 score[at, across] = both * lanes ** (-0.5)
             return carry
 
-        def means(source_head, carry):
-            arrived(u, source_head, (2,))
+        def average(n, carry):
+            source_head = lax.rem(n, heads)
+            place = u * each * blocks + n // heads
+            source_part = place // blocks
+
+            @pl.when(elsewhere(source_head, source_part))
+            def _():
+                pltpu.make_async_remote_copy(
+                    src_ref=code.at[0, pl.ds(0, rows)],
+                    dst_ref=code_in.at[source_head, pl.ds(pl.multiple_of(place * rows, rows), rows)],
+                    send_sem=code_send.at[0],
+                    recv_sem=code_recv.at[source_head * ratio + source_part, lax.rem(place, blocks)],
+                    device_id=(source_head, head * ratio + source_part),
+                    device_id_type=MESH,
+                ).wait_recv()
 
             def decode(c, carry):
-                at = place_of(c)
+                at = pl.ds(pl.multiple_of(place * rows + c * slab, slab), slab)
                 level = code_in[source_head, at, :].astype(jnp.int32).astype(jnp.float32)
                 share = jnp.exp2((jnp.abs(level) - TOP) * (SPAN / TOP))
                 share = jnp.where(level == 0.0, 0.0, jnp.where(level < 0.0, -share, share))
                 mean[source_head, at, :] = mean[source_head, at, :] * share
                 return carry
 
-            lax.fori_loop(0, unit_rows // slab, decode, 0)
+            lax.fori_loop(0, rows // slab, decode, 0)
             return carry
 
-        lax.fori_loop(0, heads, bounds, 0)
-        lax.fori_loop(0, heads, means, 0)
+        lax.fori_loop(0, heads, spread, 0)
+        lax.fori_loop(0, heads * each * blocks, average, 0)
         return carry
 
     lax.fori_loop(0, owned // unit, finish, 0)
@@ -296,20 +328,23 @@
     def sent(step, carry):
         @pl.when(jnp.logical_not(jnp.logical_and(mine, dest_of(step) == seq)))
         def _():
-            for k in range(3):
-                remote(step, k).wait_send()
+            block_code(step).wait_send()
+
+            @pl.when(lax.rem(step, blocks) == 0)
+            def _():
+                whole_bounds(step).wait_send()
 
         return carry
 
     lax.fori_loop(0, steps, sent, 0)
 
 
-def store_kernel(low, high, mean, score, low_out, high_out, mean_out, score_out, sem):
-    heads = low.shape[0]
+def store_kernel(bounds, mean, score, low_out, high_out, mean_out, score_out, sem):
     copies = []
-    for k, (source, target) in enumerate(((mean, mean_out), (low, low_out), (high, high_out))):
-        for head in range(heads):
-            copies.append(pltpu.make_async_copy(source.at[head], target.at[:, head], sem.at[k, head]))
+    for head in range(bounds.shape[0]):
+        copies.append(pltpu.make_async_copy(mean.at[head], mean_out.at[:, :, head], sem.at[0, head]))
+        for k, target in ((0, low_out), (1, high_out)):
+            copies.append(pltpu.make_async_copy(bounds.at[head, :, k], target.at[:, :, head], sem.at[1 + k, head]))
     copies.append(pltpu.make_async_copy(score, score_out, sem.at[3, 0]))
     for copy in copies:
         copy.start()
@@ -326,37 +361,38 @@
     count_q = heads * local_q
     block = min(BLOCK, pages)
     blocks = pages // block
-    unit = min(UNIT, owned)
+    unit = min(max(LANE, pages), owned)
     tall = PAGE * width
     keys = cached_keys.reshape(seq_count, pages, tall, lanes)
     vmem = pl.BlockSpec(memory_space=pltpu.VMEM)
     hbm = pl.BlockSpec(memory_space=pltpu.HBM)
     shape = (heads, owned * width, lanes)
-    sends = (seqs * blocks, block * width, lanes)
-    low, high, mean, score = pl.pallas_call(
+    ratio = seqs // heads
+    message = pages * width
+    bounds, mean, score = pl.pallas_call(
         functools.partial(page_kernel, seqs, heads),
         out_shape=(
-            pltpu.VMEM(shape, jnp.bfloat16),
-            pltpu.VMEM(shape, jnp.bfloat16),
+            pltpu.VMEM((heads, ratio, 2, message, lanes), jnp.bfloat16),
             pltpu.VMEM(shape, jnp.float32),
             pltpu.VMEM((count_q, owned), jnp.float32),
         ),
         in_specs=[hbm] * 3,
-        out_specs=(vmem,) * 4,
+        out_specs=(vmem,) * 3,
         scratch_shapes=[
             pltpu.SMEM((seq_count,), jnp.int32),
             pltpu.VMEM((SLOTS, block, tall, lanes), jnp.bfloat16),
-            pltpu.VMEM(sends, jnp.bfloat16),
-            pltpu.VMEM(sends, jnp.bfloat16),
-            pltpu.VMEM(sends, jnp.int16),
+            pltpu.VMEM((seqs, 2, message, lanes), jnp.bfloat16),
+            pltpu.VMEM((seqs, message, lanes), jnp.int16),
             pltpu.VMEM(shape, jnp.int16),
             pltpu.VMEM((heads, local_q, lanes), jnp.bfloat16),
             pltpu.VMEM((unit * width, lanes), jnp.float32),
             pltpu.VMEM((unit * width, lanes), jnp.float32),
             pltpu.VMEM((count_q, lanes), jnp.float32),
             pltpu.SemaphoreType.DMA((SLOTS,)),
-            pltpu.SemaphoreType.DMA((seqs * blocks, 3)),
-            pltpu.SemaphoreType.DMA((seqs, blocks, 3)),
+            pltpu.SemaphoreType.DMA((seqs,)),
+            pltpu.SemaphoreType.DMA((seqs,)),
+            pltpu.SemaphoreType.DMA((seqs * blocks,)),
+            pltpu.SemaphoreType.DMA((seqs, blocks)),
             pltpu.SemaphoreType.DMA((heads - 1,)),
             pltpu.SemaphoreType.DMA((heads - 1,)),
             pltpu.SemaphoreType.DMA,
@@ -369,8 +405,7 @@
         pltpu.with_memory_space_constraint(keys, pltpu.HBM),
         pltpu.with_memory_space_constraint(queries.reshape(local_q, lanes), pltpu.HBM),
     )
-    split = (heads, owned, width, lanes)
-    whole = (owned, heads, width, lanes)
+    whole = (ratio, pages, heads, width, lanes)
     low, high, mean, score = pl.pallas_call(
         store_kernel,
         out_shape=(
@@ -379,12 +414,16 @@
             jax.ShapeDtypeStruct(whole, jnp.float32),
             jax.ShapeDtypeStruct((count_q, owned), jnp.float32),
         ),
-        in_specs=[vmem] * 4,
+        in_specs=[vmem] * 3,
         out_specs=(hbm,) * 4,
         scratch_shapes=[pltpu.SemaphoreType.DMA((4, heads))],
         compiler_params=pltpu.CompilerParams(vmem_limit_bytes=16 << 20),
         name="page_store",
-    )(low.reshape(split), high.reshape(split), mean.reshape(split), score)
+    )(
+        bounds.reshape(heads, ratio, 2, pages, width, lanes),
+        mean.reshape(heads, ratio, pages, width, lanes),
+        score,
+    )
     final = (1, owned, kv_heads, lanes)
     return low.reshape(final), high.reshape(final), mean.reshape(final), score.reshape(1, count_q, owned)
 

time: 78.2 us -> 77.7 us (level)
  no operation moved by 1% of the time
where the time goes in v4:
time: 77.7 us; the launch traced here: 76.8 us
  Pallas kernels  76.1 us (98%)
    pallas_call x1, Pallas kernels, local_step(): pl.pallas_call(functools.partial(page_kernel, seqs, heads), out_shape=(pl...  74 us
    pallas_call x1, Pallas kernels, local_step(): pl.pallas_call(store_kernel, out_shape=(jax.ShapeDtypeStruct(whole, jnp.b...  2.18 us

profile of v4, /device:TPU:19, one launch (start us, length us, event | category | flops | bytes accessed | tf_op | source)
XLA Modules:
  0.0 76.8 jit_solution(13972347628492874366)
XLA Ops:
  0.6 74.0 %page_exchange.1 = (bf16[4,2,2,512,128]{4,3,2,1,0:T(8,128)(2,1)S(1)}, f32[4,1024,128]{2,1,0:T(8,128)S(1)}, f32[64,512]{1,0:T(8,128)S(1)}) custom-call(s32[8]{0:T(128)} %lengths_hbm.1, bf16[8,256,32,128]{3,2,1,0:T(8,128)(2,1)} %bitcast.10, bf16[16,128]{1,0:T(8,128)(2,1)} %bitcast.11), custom_call_target="tpu_custom_call" | custom-call | tf_op jit(solution)/shard_map/page_exchange/pallas_call | solution.py:372
  74.6 2.2 %page_store.1 = (bf16[2,256,4,2,128]{4,3,2,1,0:T(2,128)(2,1)}, bf16[2,256,4,2,128]{4,3,2,1,0:T(2,128)(2,1)}, f32[2,256,4,2,128]{4,3,2,1,0:T(2,128)}, f32[64,512]{1,0:T(8,128)}) custom-call(bf16[4,2,2,256,2,128]{5,4,3,2,1,0:T(2,128)(2,1)S(1)} %bitcast.8, f32[4,2,256,2,128]{4,3,2,1,0:T(2,128)S(1)} %bitcast.9, f32[64,512]{1,0:T(8,128)S(1)} %get-tuple-element.13.score), custom_call_target="tpu_custom_call" | custom-call | tf_op jit(solution)/shard_map/page_store/pallas_call | solution.py:409

commit v5 on v4

--- a/solution.py
+++ b/solution.py
@@ -130,8 +130,18 @@
         return pltpu.make_async_remote_copy(
             src_ref=code.at[step // blocks, inside_of(step)],
             dst_ref=code_in.at[head, landing(step)],
-            send_sem=code_send.at[step],
-            recv_sem=code_recv.at[index, lax.rem(step, blocks)],
+            send_sem=code_send.at[step // blocks],
+            recv_sem=code_recv.at[index],
+            device_id=(owner, dest_of(step)),
+            device_id_type=MESH,
+        )
+
+    def whole_code(step):
+        return pltpu.make_async_remote_copy(
+            src_ref=code.at[step // blocks],
+            dst_ref=code_in.at[head, pl.ds(pl.multiple_of(part * pages * width, pages * width), pages * width)],
+            send_sem=code_send.at[step // blocks],
+            recv_sem=code_recv.at[index],
             device_id=(owner, dest_of(step)),
             device_id_type=MESH,
         )
@@ -214,8 +224,7 @@
         @pl.when(jnp.logical_and(jnp.logical_not(itself), complete))
         def _():
             whole_bounds(step).start()
-            for b in range(blocks):
-                block_code(step - (blocks - 1) + b).start()
+            whole_code(step).start()
 
         return carry
 
@@ -294,33 +303,32 @@
 
         def average(n, carry):
             source_head = lax.rem(n, heads)
-            place = u * each * blocks + n // heads
-            source_part = place // blocks
+            source_part = u * each + n // heads
 
             @pl.when(elsewhere(source_head, source_part))
             def _():
                 pltpu.make_async_remote_copy(
-                    src_ref=code.at[0, pl.ds(0, rows)],
-                    dst_ref=code_in.at[source_head, pl.ds(pl.multiple_of(place * rows, rows), rows)],
+                    src_ref=code.at[0],
+                    dst_ref=code_in.at[source_head, pl.ds(pl.multiple_of(source_part * message, message), message)],
                     send_sem=code_send.at[0],
-                    recv_sem=code_recv.at[source_head * ratio + source_part, lax.rem(place, blocks)],
+                    recv_sem=code_recv.at[source_head * ratio + source_part],
                     device_id=(source_head, head * ratio + source_part),
                     device_id_type=MESH,
                 ).wait_recv()
 
             def decode(c, carry):
-                at = pl.ds(pl.multiple_of(place * rows + c * slab, slab), slab)
+                at = pl.ds(pl.multiple_of(source_part * message + c * slab, slab), slab)
                 level = code_in[source_head, at, :].astype(jnp.int32).astype(jnp.float32)
                 share = jnp.exp2((jnp.abs(level) - TOP) * (SPAN / TOP))
                 share = jnp.where(level == 0.0, 0.0, jnp.where(level < 0.0, -share, share))
                 mean[source_head, at, :] = mean[source_head, at, :] * share
                 return carry
 
-            lax.fori_loop(0, rows // slab, decode, 0)
+            lax.fori_loop(0, message // slab, decode, 0)
             return carry
 
         lax.fori_loop(0, heads, spread, 0)
-        lax.fori_loop(0, heads * each * blocks, average, 0)
+        lax.fori_loop(0, heads * each, average, 0)
         return carry
 
     lax.fori_loop(0, owned // unit, finish, 0)
@@ -328,11 +336,10 @@
     def sent(step, carry):
         @pl.when(jnp.logical_not(jnp.logical_and(mine, dest_of(step) == seq)))
         def _():
-            block_code(step).wait_send()
-
             @pl.when(lax.rem(step, blocks) == 0)
             def _():
                 whole_bounds(step).wait_send()
+                whole_code(step).wait_send()
 
         return carry
 
@@ -391,8 +398,8 @@
             pltpu.SemaphoreType.DMA((SLOTS,)),
             pltpu.SemaphoreType.DMA((seqs,)),
             pltpu.SemaphoreType.DMA((seqs,)),
-            pltpu.SemaphoreType.DMA((seqs * blocks,)),
-            pltpu.SemaphoreType.DMA((seqs, blocks)),
+            pltpu.SemaphoreType.DMA((seqs,)),
+            pltpu.SemaphoreType.DMA((seqs,)),
             pltpu.SemaphoreType.DMA((heads - 1,)),
             pltpu.SemaphoreType.DMA((heads - 1,)),
             pltpu.SemaphoreType.DMA,

time: 77.7 us -> 77.8 us (level)
  no operation moved by 1% of the time
where the time goes in v5:
time: 77.8 us; the launch traced here: 76.8 us
  Pallas kernels  76.1 us (98%)
    pallas_call x1, Pallas kernels, local_step(): pl.pallas_call(functools.partial(page_kernel, seqs, heads), out_shape=(pl...  73.9 us
    pallas_call x1, Pallas kernels, local_step(): pl.pallas_call(store_kernel, out_shape=(jax.ShapeDtypeStruct(whole, jnp.b...  2.18 us

profile of v5, /device:TPU:19, one launch (start us, length us, event | category | flops | bytes accessed | tf_op | source)
XLA Modules:
  0.0 76.8 jit_solution(13400229224853973283)
XLA Ops:
  0.6 73.9 %page_exchange.1 = (bf16[4,2,2,512,128]{4,3,2,1,0:T(8,128)(2,1)S(1)}, f32[4,1024,128]{2,1,0:T(8,128)S(1)}, f32[64,512]{1,0:T(8,128)S(1)}) custom-call(s32[8]{0:T(128)} %lengths_hbm.1, bf16[8,256,32,128]{3,2,1,0:T(8,128)(2,1)} %bitcast.10, bf16[16,128]{1,0:T(8,128)(2,1)} %bitcast.11), custom_call_target="tpu_custom_call" | custom-call | tf_op jit(solution)/shard_map/page_exchange/pallas_call | solution.py:379
  74.6 2.2 %page_store.1 = (bf16[2,256,4,2,128]{4,3,2,1,0:T(2,128)(2,1)}, bf16[2,256,4,2,128]{4,3,2,1,0:T(2,128)(2,1)}, f32[2,256,4,2,128]{4,3,2,1,0:T(2,128)}, f32[64,512]{1,0:T(8,128)}) custom-call(bf16[4,2,2,256,2,128]{5,4,3,2,1,0:T(2,128)(2,1)S(1)} %bitcast.8, f32[4,2,256,2,128]{4,3,2,1,0:T(2,128)S(1)} %bitcast.9, f32[64,512]{1,0:T(8,128)S(1)} %get-tuple-element.13.score), custom_call_target="tpu_custom_call" | custom-call | tf_op jit(solution)/shard_map/page_store/pallas_call | solution.py:416
